TPU v7x, 32 devices: a whole 2x2x4 slice. The times are simulated.
32 devices in a mesh: dp: 2 (over x), expert: 16 (over z, y, core).
Axes of the slice: x: 2, y: 2, z: 4, core: 2. Of those that a mesh axis runs over, the one named last changes fastest.
Arguments:
- tokens: bfloat16 [256, 2048], P(('dp', 'expert')), may hold values from -6 to 6
- out_grad: bfloat16 [256, 2048], P(('dp', 'expert')), may hold values from -6 to 6
- expert_ids: int32 [256, 8], P(('dp', 'expert')), may hold values from 0 to 15, all different within a row; in each aligned block of 8 rows (0 to 7, 8 to 15, ...) at most 8 rows name the same one
- gate_values: float32 [256, 8], P(('dp', 'expert')), may hold values from 0.05 to 1
- w_gate: bfloat16 [16, 2048, 1024], P('expert', None, 'dp'), may hold values from -0.125 to 0.125
- w_up: bfloat16 [16, 2048, 1024], P('expert', None, 'dp'), may hold values from -0.125 to 0.125
- w_down: bfloat16 [16, 1024, 2048], P('expert', 'dp'), may hold values from -0.1875 to 0.1875
Outputs:
- grad_tokens: bfloat16 [256, 2048], P(('dp', 'expert'))
- grad_gate: float32 [16, 2048, 1024], P('expert', None, 'dp')
- grad_up: float32 [16, 2048, 1024], P('expert', None, 'dp')
- grad_down: float32 [16, 1024, 2048], P('expert', 'dp')
Inputs may be any that keep to these rules, and one draw needn't show every extreme that they name: `expert_ids`: each token names 8 different experts. Among the 8 tokens of one device (aligned blocks of 8 rows) no expert is named more than 8 times, and in every draw some expert is named exactly 8 times in some block.
All inputs are finite; a program needn't handle non-finite values.
Results may differ from a plain program's by a relative error of at most 0.014.
Values may be sent and summed in bfloat16 or wider, within the bound.
No kernel may reach another device: no remote copies, remote signals or barrier semaphores. Data moves between devices by JAX's collectives and lax.ppermute only.
A program may use at most 64 MiB of HBM per device.

v0:
```python
import jax
import jax.numpy as jnp
from jax import lax
from jax.sharding import PartitionSpec as P


def contract_last(left_op, right_op):
    return lax.dot_general(
        left_op, right_op, (((1,), (1,)), ((), ())), preferred_element_type=jnp.float32
    )


def contract_first(left_op, right_op):
    return lax.dot_general(
        left_op, right_op, (((0,), (0,)), ((), ())), preferred_element_type=jnp.float32
    )


def slot_table(expert_ids, gate_values, expert_count, capacity):
    tok_rows, top_count = expert_ids.shape
    flat_ids = expert_ids.reshape(-1)
    onehot = (flat_ids[:, None] == jnp.arange(expert_count, dtype=jnp.int32)[None, :]).astype(
        jnp.int32
    )
    before = jnp.cumsum(onehot, axis=0) - onehot
    slot_rank = jnp.sum(before * onehot, axis=1)
    slot_index = flat_ids * capacity + slot_rank
    slot_hits = (
        slot_index[:, None] == jnp.arange(expert_count * capacity, dtype=jnp.int32)[None, :]
    ).astype(jnp.float32)
    owner_row = jnp.arange(tok_rows * top_count, dtype=jnp.int32) // top_count
    token_hits = (owner_row[:, None] == jnp.arange(tok_rows, dtype=jnp.int32)[None, :]).astype(
        jnp.float32
    )
    weighted = slot_hits * gate_values.reshape(-1)[:, None]
    return jnp.dot(weighted.T, token_hits, precision=lax.Precision.HIGHEST)


def expert_backward(x_rows, g_rows, w_pair, w_back):
    hidden_units = w_back.shape[0]
    pair_out = jnp.dot(x_rows, w_pair, preferred_element_type=jnp.float32)
    gate_pre = pair_out[:, :hidden_units]
    up_pre = pair_out[:, hidden_units:]
    sigmoid_val = jax.nn.sigmoid(gate_pre)
    silu_val = gate_pre * sigmoid_val
    activation = (silu_val * up_pre).astype(jnp.bfloat16)
    act_grad = contract_last(g_rows, w_back)
    up_grad = (act_grad * silu_val).astype(jnp.bfloat16)
    gate_grad = (act_grad * up_pre * sigmoid_val * (1.0 + gate_pre * (1.0 - sigmoid_val))).astype(
        jnp.bfloat16
    )
    pair_grads = jnp.concatenate([gate_grad, up_grad], axis=1)
    weight_pair_grad = contract_first(x_rows, pair_grads)
    weight_back_grad = contract_first(activation, g_rows)
    return (pair_grads, weight_pair_grad, weight_back_grad)


def shards(tokens, out_grad, expert_ids, gate_values, w_gate, w_up, w_down):
    expert_count = lax.axis_size("expert")
    tok_rows = tokens.shape[0]
    top_count = expert_ids.shape[1]
    model_width = tokens.shape[1]
    capacity = 2 * tok_rows * top_count // expert_count
    slot_count = expert_count * capacity
    hidden_units = w_down.shape[1]
    gate_table = slot_table(expert_ids, gate_values, expert_count, capacity)
    w_pair = jnp.concatenate([w_gate[0], w_up[0]], axis=1)
    w_back = w_down[0]
    pick_table = (gate_table > 0.0).astype(jnp.bfloat16)
    sent_rows = jnp.dot(pick_table, tokens, preferred_element_type=jnp.float32).astype(jnp.bfloat16)
    sent_grads = jnp.dot(
        gate_table, out_grad.astype(jnp.float32), precision=lax.Precision.HIGHEST
    ).astype(jnp.bfloat16)
    got_rows, got_grads = (
        lax.all_to_all(
            sent_rows.reshape(expert_count, capacity, model_width),
            "expert",
            split_axis=0,
            concat_axis=0,
            tiled=True,
        ),
        lax.all_to_all(
            sent_grads.reshape(expert_count, capacity, model_width),
            "expert",
            split_axis=0,
            concat_axis=0,
            tiled=True,
        ),
    )
    local_rows = got_rows.reshape(slot_count, model_width)
    local_grads = got_grads.reshape(slot_count, model_width)
    part_rows = lax.all_gather(local_rows, "dp", axis=0, tiled=True)
    part_grads = lax.all_gather(local_grads, "dp", axis=0, tiled=True)
    pair_part, pair_term, back_term = expert_backward(part_rows, part_grads, w_pair, w_back)
    own_sums = lax.psum_scatter(
        contract_last(pair_part, w_pair).astype(jnp.bfloat16), "dp", scatter_dimension=0, tiled=True
    ).astype(jnp.float32)
    back_rows = lax.all_to_all(
        own_sums.reshape(expert_count, capacity, model_width).astype(jnp.bfloat16),
        "expert",
        split_axis=0,
        concat_axis=0,
        tiled=True,
    ).astype(jnp.float32)
    pick_float = (gate_table > 0.0).astype(jnp.float32)
    token_grad = jnp.dot(
        pick_float.T, back_rows.reshape(slot_count, model_width), precision=lax.Precision.HIGHEST
    )
    grad_tokens = token_grad.astype(jnp.bfloat16)
    grad_gate = pair_term[:, :hidden_units][None]
    grad_up = pair_term[:, hidden_units:][None]
    grad_down = back_term[None]
    return (grad_tokens, grad_gate, grad_up, grad_down)


def solution(mesh):
    return jax.shard_map(
        shards,
        mesh=mesh,
        in_specs=(
            P(("dp", "expert"), None),
            P(("dp", "expert"), None),
            P(("dp", "expert"), None),
            P(("dp", "expert"), None),
            P("expert", None, "dp"),
            P("expert", None, "dp"),
            P("expert", "dp", None),
        ),
        out_specs=(
            P(("dp", "expert"), None),
            P("expert", None, "dp"),
            P("expert", None, "dp"),
            P("expert", "dp", None),
        ),
        check_vma=False,
    )
```

profile of v0, /device:TPU:0, one launch (start us, length us, event | category | flops | bytes accessed | tf_op | source)
XLA Modules:
  0.0 129.1 jit_solution(14896690260324359717)
XLA Ops:
  7.2 0.9 reshape.51
  8.1 0.1 fusion.13
  8.2 0.1 reduce_window_sum.11
  8.3 0.2 select_reduce_fusion
  8.5 0.8 mul.47
  9.3 0.3 broadcast_compare_fusion
  9.5 1.1 fusion.4
  10.7 21.6 %all_to_all.15 = bf16[16,8,2048]{2,1,0:T(8,128)(2,1)} all-to-all(bf16[16,8,2048]{2,1,0:T(8,128)(2,1)S(1)} %fusion.4), channel_id=1, replica_groups=mesh['dp'=2,'expert'=16] {'expert'}, dimensions={0} | all-to-all | bytes 1048576 | tf_op jit(solution)/shard_map/all_to_all | solution.py:75
  32.3 1.4 %fusion.3 = bf16[16,8,2048]{2,1,0:T(8,128)(2,1)S(1)} fusion(f32[128,8]{0,1:T(8,128)S(1)} %get-tuple-element.9, bf16[8,2048]{1,0:T(8,128)(2,1)} %param.8), kind=kOutput, calls=%fused_computation.9 | convolution fusion | flops 25427968 | bytes 561152 | tf_op jit(solution)/shard_map/dot_general | solution.py:71
  33.7 18.3 %all_to_all.16 = bf16[16,8,2048]{2,1,0:T(8,128)(2,1)} all-to-all(bf16[16,8,2048]{2,1,0:T(8,128)(2,1)S(1)} %fusion.3), channel_id=1, replica_groups=mesh['dp'=2,'expert'=16] {'expert'}, dimensions={0} | all-to-all | bytes 1048576 | tf_op jit(solution)/shard_map/all_to_all | solution.py:82
  52.1 0.0 reduce-scatter.2.cloned.1.call-start
  52.1 1.1 all-gather.5.cloned.1.call-done
  53.2 3.8 %fusion.1 = f32[256,1024]{1,0:T(8,128)S(1)} fusion(bf16[256,2048]{1,0:T(8,128)(2,1)} %all-gather.5.cloned.1.call-done, bf16[2048,512]{1,0:T(8,128)(2,1)} %bitcast.35, bf16[2048,512]{1,0:T(8,128)(2,1)} %bitcast.37), kind=kOutput, calls=%fused_computation.5 | convolution fusion | flops 1082130432 | bytes 6291456 | tf_op jit(solution)/shard_map/dot_general | solution.py:41
  57.0 19.0 %all-gather.3.cloned.1.call-done = bf16[256,2048]{1,0:T(8,128)(2,1)} async-done(((bf16[128,2048]{1,0:T(8,128)(2,1)}), bf16[256,2048]{1,0:T(8,128)(2,1)}) %all-gather.3.cloned.1.call-update) | async-done | bytes 1048592 | tf_op jit(solution)/shard_map/all_gather | solution.py:93
  76.1 2.2 %multiply_convert_fusion.2 = (bf16[256,512]{1,0:T(8,128)(2,1)S(1)}, bf16[256,512]{1,0:T(8,128)(2,1)S(1)}) fusion(f32[256,1024]{1,0:T(8,128)S(1)} %fusion.1, bf16[256,2048]{1,0:T(8,128)(2,1)} %all-gather.3.cloned.1.call-done, bf16[1,512,2048]{2,1,0:T(8,128)(2,1)S(1)} %copy-done), kind=kOutput, calls=%fused_computation.18 | convolution fusion | flops 538574848 | bytes 4718592 | tf_op jit(solution)/shard_map/dot_general | solution.py:8
  78.4 0.7 copy-done.2
  79.0 2.3 %fusion.2 = bf16[256,2048]{1,0:T(8,128)(2,1)} fusion(bf16[2048,512]{1,0:T(8,128)(2,1)S(1)} %bitcast.36, bf16[2048,512]{1,0:T(8,128)(2,1)S(1)} %bitcast.38, bf16[256,512]{1,0:T(8,128)(2,1)S(1)} %get-tuple-element.7, bf16[256,512]{1,0:T(8,128)(2,1)S(1)} %get-tuple-element.6), kind=kOutput, calls=%fused_computation.6 | convolution fusion | flops 1083703296 | bytes 5767168 | tf_op jit(solution)/shard_map/dot_general | solution.py:8
  81.4 5.5 %fusion.9 = f32[2048,1024]{1,0:T(8,128)} fusion(bf16[256,2048]{1,0:T(8,128)(2,1)S(1)} %copy-done.1, bf16[256,512]{1,0:T(8,128)(2,1)} %copy-done.2, bf16[256,512]{1,0:T(8,128)(2,1)S(1)} %get-tuple-element.6), kind=kOutput, calls=%fused_computation.21 | convolution fusion | flops 1074790400 | bytes 9961472 | tf_op jit(solution)/shard_map/dot_general | solution.py:14
  86.8 15.1 %reduce-scatter.2.cloned.1.call-done = bf16[128,2048]{1,0:T(8,128)(2,1)} async-done(((bf16[256,2048]{1,0:T(8,128)(2,1)}), bf16[128,2048]{1,0:T(8,128)(2,1)}) %reduce-scatter.2.cloned.1.call-update) | async-done | bytes 524304 | tf_op jit(solution)/shard_map/reduce_scatter | solution.py:95
  101.9 5.6 %all-to-all-start.2 = ((bf16[16,8,2048]{2,1,0:T(8,128)(2,1)}), bf16[16,8,2048]{2,1,0:T(8,128)(2,1)S(1)}, u32[]{:S(2)}, u32[]{:S(2)}) async-start(bf16[16,8,2048]{2,1,0:T(8,128)(2,1)} %bitcast.34), calls=%async_computation.3 | async-start | bytes 1048576 | tf_op jit(solution)/shard_map/all_to_all | solution.py:98
  107.5 4.4 %convolution_bitcast_fusion = f32[1,512,2048]{2,1,0:T(8,128)} fusion(bf16[256,2048]{1,0:T(8,128)(2,1)} %all-gather.3.cloned.1.call-done, f32[256,1024]{1,0:T(8,128)} %copy-done.5), kind=kOutput, calls=%fused_computation.3 | convolution fusion | flops 537657344 | bytes 6291456 | tf_op jit(solution)/shard_map/dot_general | solution.py:14
  111.9 7.8 %slice_bitcast_fusion = (f32[1,2048,512]{2,1,0:T(8,128)}, f32[1,2048,512]{2,1,0:T(8,128)}) fusion(f32[2048,1024]{1,0:T(8,128)} %fusion.9), kind=kLoop, calls=%fused_computation | loop fusion | bytes 16777216 | tf_op jit(solution)/shard_map/broadcast_in_dim | solution.py:111
  119.7 2.1 %all-to-all-done.2 = bf16[16,8,2048]{2,1,0:T(8,128)(2,1)S(1)} async-done(((bf16[16,8,2048]{2,1,0:T(8,128)(2,1)}), bf16[16,8,2048]{2,1,0:T(8,128)(2,1)S(1)}, u32[]{:S(2)}, u32[]{:S(2)}) %all-to-all-start.2) | async-done | bytes 524320 | tf_op jit(solution)/shard_map/all_to_all | solution.py:98
  121.8 0.8 convolution_convert_fusion.2
  (17 shorter events, 0.2 us)
Async XLA Ops:
  7.2 68.9 %copy-start = (bf16[1,512,2048]{2,1,0:T(8,128)(2,1)S(1)}, bf16[1,512,2048]{2,1,0:T(8,128)(2,1)}, u32[]{:S(2)}) copy-start(bf16[1,512,2048]{2,1,0:T(8,128)(2,1)} %param.13) | copy-start | bytes 6291460
  7.2 46.0 %all-gather.5.cloned.1.call-start = ((), (), s32[]{:S(2)}) async-start(), calls=%async_computation.5 | async-start | bytes 1572864 | tf_op jit(solution)/shard_map/all_gather | solution.py:92
  32.3 43.8 %all-gather.3.cloned.1.call-start = ((), (), s32[]{:S(2)}) async-start(), calls=%async_computation.4 | async-start | bytes 1572864 | tf_op jit(solution)/shard_map/all_gather | solution.py:93
  52.1 49.8 %reduce-scatter.2.cloned.1.call-start = ((), (), s32[]{:S(2)}) async-start(), calls=%async_computation.6 | async-start | bytes 1572864 | tf_op jit(solution)/shard_map/reduce_scatter | solution.py:95
  57.0 21.3 %copy-start.5 = (f32[256,1024]{1,0:T(8,128)}, f32[256,1024]{1,0:T(8,128)S(1)}, u32[]{:S(2)}) copy-start(f32[256,1024]{1,0:T(8,128)S(1)} %fusion.1) | copy-start | bytes 3145732
  76.1 3.0 %copy-start.3 = (bf16[1,2048,512]{2,1,0:T(8,128)(2,1)S(1)}, bf16[1,2048,512]{2,1,0:T(8,128)(2,1)}, u32[]{:S(2)}) copy-start(bf16[1,2048,512]{2,1,0:T(8,128)(2,1)} %param.12) | copy-start | bytes 6291460
  76.1 3.0 %copy-start.4 = (bf16[1,2048,512]{2,1,0:T(8,128)(2,1)S(1)}, bf16[1,2048,512]{2,1,0:T(8,128)(2,1)}, u32[]{:S(2)}) copy-start(bf16[1,2048,512]{2,1,0:T(8,128)(2,1)} %param.11) | copy-start | bytes 6291460
  78.3 0.7 copy-start.2
  79.0 2.3 %copy-start.1 = (bf16[256,2048]{1,0:T(8,128)(2,1)S(1)}, bf16[256,2048]{1,0:T(8,128)(2,1)}, u32[]{:S(2)}) copy-start(bf16[256,2048]{1,0:T(8,128)(2,1)} %all-gather.5.cloned.1.call-done) | copy-start | bytes 3145732
  101.9 19.9 %all-to-all-start.2 = ((bf16[16,8,2048]{2,1,0:T(8,128)(2,1)}), bf16[16,8,2048]{2,1,0:T(8,128)(2,1)S(1)}, u32[]{:S(2)}, u32[]{:S(2)}) async-start(bf16[16,8,2048]{2,1,0:T(8,128)(2,1)} %bitcast.34), calls=%async_computation.3 | async-start | bytes 1048576 | tf_op jit(solution)/shard_map/all_to_all | solution.py:98
Sparse Core Ops, SparseCore 0:
  32.4 20.7 all-gather.4
  54.8 21.2 all-gather.2
  81.5 20.3 reduce-scatter.1
where the time goes:
time: 130 us; the launch traced here: 129 us
  blocking collectives  39.9 us (31%)
  waiting for transfers between devices  37.3 us (29%)
  matrix products  21.7 us (17%)
  between operations  13.8 us (11%)
  local copies, waits for them, and re-layouts  10.2 us (8%)
  starting transfers between devices  5.74 us (4%)
    all_to_all x1, blocking collectives, shards(): lax.all_to_all(sent_rows.reshape(expert_count, capacity, model_width), 'e...  21.6 us
    all_gather x1, waiting for transfers between devices, shards(): part_grads = lax.all_gather(local_grads, 'dp', axis=0, tiled=True)  19 us
    all_to_all x1, blocking collectives, shards(): lax.all_to_all(sent_grads.reshape(expert_count, capacity, model_width), '...  18.3 us
    reduce_scatter x1, waiting for transfers between devices, shards(): lax.psum_scatter(contract_last(pair_part, w_pair).astype(jnp.bfloat16), '...  15.1 us
    dot_general x2, matrix products, contract_first(): lax.dot_general(left_op, right_op, (((0,), (0,)), ((), ())), preferred_el...  9.81 us
    broadcast_in_dim x1, local copies, waits for them, and re-layouts, shards(): grad_up = pair_term[:, hidden_units:][None]  7.84 us
    all_to_all x1, starting transfers between devices, shards(): lax.all_to_all(own_sums.reshape(expert_count, capacity, model_width).asty...  5.62 us
    dot_general x2, matrix products, contract_last(): lax.dot_general(left_op, right_op, (((1,), (1,)), ((), ())), preferred_el...  4.52 us
  transfers between devices with their start and end apart: 4, of which 4 were waited for; matrix products, arithmetic and copies ran while one was open for 18% of the time, Pallas kernels for 0%

commit v1 on v0

v1 whole, which is shorter than its diff:
```python
import jax
import jax.numpy as jnp
from jax import lax
from jax.sharding import PartitionSpec as P

AXES = ("dp", "expert")


def contract_last(left_op, right_op):
    return lax.dot_general(
        left_op, right_op, (((1,), (1,)), ((), ())), preferred_element_type=jnp.float32
    )


def contract_first(left_op, right_op):
    return lax.dot_general(
        left_op, right_op, (((0,), (0,)), ((), ())), preferred_element_type=jnp.float32
    )


def contract_inner(left_op, right_op):
    return jnp.dot(left_op, right_op, preferred_element_type=jnp.float32)


def hidden_grads(gate_pre, up_pre, act_grad):
    sigmoid_val = jax.nn.sigmoid(gate_pre)
    silu_val = gate_pre * sigmoid_val
    activation = (silu_val * up_pre).astype(jnp.bfloat16)
    up_grad = (act_grad * silu_val).astype(jnp.bfloat16)
    gate_grad = (act_grad * up_pre * sigmoid_val * (1.0 + gate_pre * (1.0 - sigmoid_val))).astype(
        jnp.bfloat16
    )
    return activation, gate_grad, up_grad


def exchange_stages(device_count):
    top = device_count // 2
    far = [bit for bit in (1 << i for i in range(2, 32)) if bit < top]
    masks = [0]
    for bit in far:
        masks = masks + [mask | bit for mask in masks]
    return [[(mask, mask) for mask in masks[1:]], [(2, top)], [(top, 2)], [(1, 1)]]


def swap(value, masks, device_count):
    even, odd = masks
    pairs = [(i, i ^ (odd if i % 2 else even)) for i in range(device_count)]
    return lax.ppermute(value, AXES, pairs)


def gate_columns(expert_ids, gate_values, expert_count, width):
    named = expert_ids[:, :, None] == jnp.arange(expert_count, dtype=jnp.int32)[None, None, :]
    weight = jnp.sum(jnp.where(named, gate_values[:, :, None], 0.0), axis=1)
    high = lax.reduce_precision(weight, 8, 7)
    middle = lax.reduce_precision(weight - high, 8, 7)
    low = weight - high - middle
    pieces = jnp.concatenate([high, middle, low], axis=1)
    return jnp.pad(pieces, ((0, 0), (0, width - pieces.shape[1]))).astype(jnp.bfloat16)


def all_rows(tokens, out_grad, expert_ids, gate_values, w_gate, w_up, w_down):
    expert_count = lax.axis_size("expert")
    device_count = lax.axis_size("dp") * expert_count
    model_width = tokens.shape[1]
    gate_width = -(-3 * expert_count // 128) * 128
    stages = exchange_stages(device_count)
    rows = jnp.concatenate(
        [tokens, out_grad, gate_columns(expert_ids, gate_values, expert_count, gate_width)], axis=1
    )
    for stage in stages:
        rows = jnp.concatenate([rows] + [swap(rows, mask, device_count) for mask in stage], axis=0)
    x_rows = rows[:, :model_width]
    pieces = rows[:, 2 * model_width :].astype(jnp.float32)
    column = jnp.arange(gate_width, dtype=jnp.int32)[None, :]
    mine = (column % expert_count == lax.axis_index("expert")) & (column < 3 * expert_count)
    gate = jnp.sum(jnp.where(mine, pieces, 0.0), axis=1, keepdims=True)
    g_rows = (gate * rows[:, model_width : 2 * model_width].astype(jnp.float32)).astype(
        jnp.bfloat16
    )
    activation, gate_grad, up_grad = hidden_grads(
        contract_inner(x_rows, w_gate[0]),
        contract_inner(x_rows, w_up[0]),
        contract_last(g_rows, w_down[0]),
    )
    sums = contract_last(gate_grad, w_gate[0]) + contract_last(up_grad, w_up[0])
    sums = sums.astype(jnp.bfloat16)
    for stage in reversed(stages):
        parts = jnp.split(sums, len(stage) + 1, axis=0)
        total = parts[0].astype(jnp.float32)
        for part, mask in zip(parts[1:], stage):
            total = total + swap(part, mask, device_count).astype(jnp.float32)
        sums = total.astype(jnp.bfloat16)
    grad_gate = contract_first(x_rows, gate_grad)
    grad_up = contract_first(x_rows, up_grad)
    grad_down = contract_first(activation, g_rows)
    return sums, grad_gate[None], grad_up[None], grad_down[None]


def slot_table(expert_ids, gate_values, expert_count, capacity):
    tok_rows, top_count = expert_ids.shape
    flat_ids = expert_ids.reshape(-1)
    onehot = (flat_ids[:, None] == jnp.arange(expert_count, dtype=jnp.int32)[None, :]).astype(
        jnp.int32
    )
    before = jnp.cumsum(onehot, axis=0) - onehot
    slot_rank = jnp.sum(before * onehot, axis=1)
    slot_index = flat_ids * capacity + slot_rank
    slot_hits = (
        slot_index[:, None] == jnp.arange(expert_count * capacity, dtype=jnp.int32)[None, :]
    ).astype(jnp.float32)
    owner_row = jnp.arange(tok_rows * top_count, dtype=jnp.int32) // top_count
    token_hits = (owner_row[:, None] == jnp.arange(tok_rows, dtype=jnp.int32)[None, :]).astype(
        jnp.float32
    )
    weighted = slot_hits * gate_values.reshape(-1)[:, None]
    return jnp.dot(weighted.T, token_hits, precision=lax.Precision.HIGHEST)


def slot_rows(tokens, out_grad, expert_ids, gate_values, w_gate, w_up, w_down):
    expert_count = lax.axis_size("expert")
    tok_rows, model_width = tokens.shape
    capacity = slots_of(expert_ids.shape, expert_count)
    slot_count = expert_count * capacity
    gate_table = slot_table(expert_ids, gate_values, expert_count, capacity)
    pick_table = (gate_table > 0.0).astype(jnp.float32)

    def to_experts(rows):
        return lax.all_to_all(
            rows.reshape(expert_count, capacity, model_width),
            "expert",
            split_axis=0,
            concat_axis=0,
            tiled=True,
        ).reshape(slot_count, model_width)

    sent_rows = contract_inner(pick_table.astype(jnp.bfloat16), tokens).astype(jnp.bfloat16)
    sent_grads = jnp.dot(
        gate_table, out_grad.astype(jnp.float32), precision=lax.Precision.HIGHEST
    ).astype(jnp.bfloat16)
    x_rows = lax.all_gather(to_experts(sent_rows), "dp", axis=0, tiled=True)
    g_rows = lax.all_gather(to_experts(sent_grads), "dp", axis=0, tiled=True)
    activation, gate_grad, up_grad = hidden_grads(
        contract_inner(x_rows, w_gate[0]),
        contract_inner(x_rows, w_up[0]),
        contract_last(g_rows, w_down[0]),
    )
    sums = contract_last(gate_grad, w_gate[0]) + contract_last(up_grad, w_up[0])
    own_sums = lax.psum_scatter(
        sums.astype(jnp.bfloat16), "dp", scatter_dimension=0, tiled=True
    )
    back_rows = to_experts(own_sums).astype(jnp.float32)
    token_grad = jnp.dot(pick_table.T, back_rows, precision=lax.Precision.HIGHEST)
    grad_gate = contract_first(x_rows, gate_grad)
    grad_up = contract_first(x_rows, up_grad)
    grad_down = contract_first(activation, g_rows)
    return token_grad.astype(jnp.bfloat16), grad_gate[None], grad_up[None], grad_down[None]


def slots_of(ids_shape, expert_count):
    return 2 * ids_shape[0] * ids_shape[1] // expert_count


def solution(mesh):
    dp_count, expert_count = mesh.shape["dp"], mesh.shape["expert"]
    device_count = dp_count * expert_count

    def shards(tokens, out_grad, expert_ids, gate_values, w_gate, w_up, w_down):
        capacity = slots_of(expert_ids.shape, expert_count)
        paired = device_count >= 8 and device_count & (device_count - 1) == 0
        every_row = paired and expert_count * capacity >= expert_count * tokens.shape[0]
        body = all_rows if every_row else slot_rows
        return body(tokens, out_grad, expert_ids, gate_values, w_gate, w_up, w_down)

    split = P(AXES, None)
    return jax.shard_map(
        shards,
        mesh=mesh,
        in_specs=(split, split, split, split)
        + (P("expert", None, "dp"), P("expert", None, "dp"), P("expert", "dp", None)),
        out_specs=(split, P("expert", None, "dp"), P("expert", None, "dp"), P("expert", "dp", None)),
        check_vma=False,
    )
```

time: 130 us -> 69.3 us (0.53)
  blocking collectives: 39.9 us -> 0 us
  waiting for transfers between devices: 37.3 us -> 22.6 us
  between operations: 13.8 us -> 0.8 us
  starting transfers between devices: 5.74 us -> 15.6 us
  local copies, waits for them, and re-layouts: 10.2 us -> 5.02 us
  other arithmetic: 0.36 us -> 5.23 us
  matrix products: 21.7 us -> 19.7 us
    all_to_all x2 -> x0, blocking collectives: 39.9 us -> none  [the longest x1 21.6 us: shards(): lax.all_to_all(sent_rows.reshape(expert_count, capacity, model_width), 'e...]
    ppermute x0 -> x12, waiting for transfers between devices: none -> 22.6 us  [swap(): return lax.ppermute(value, AXES, pairs)]
    all_gather x2 -> x0, waiting for transfers between devices: 20.1 us -> none  [the longest x1 19 us: shards(): part_grads = lax.all_gather(local_grads, 'dp', axis=0, tiled=True)]
    ppermute x0 -> x12, starting transfers between devices: none -> 15.6 us  [swap(): return lax.ppermute(value, AXES, pairs)]
    reduce_scatter x1 -> x0, waiting for transfers between devices: 15.1 us -> none  [shards(): lax.psum_scatter(contract_last(pair_part, w_pair).astype(jnp.bfloat16), '...]
    broadcast_in_dim x1 -> x0, local copies, waits for them, and re-layouts: 7.84 us -> none  [shards(): grad_up = pair_term[:, hidden_units:][None]]
    all_to_all x1 -> x0, starting transfers between devices: 5.62 us -> none  [shards(): lax.all_to_all(own_sums.reshape(expert_count, capacity, model_width).asty...]
    dot_general x5 -> x2, matrix products: 7.35 us -> 3.99 us  [contract_inner(): return jnp.dot(left_op, right_op, preferred_element_type=jnp.float32)]
  transfers between devices with their start and end apart: 4 -> 12, of which waited for: 4 -> 9; matrix products, arithmetic and copies ran while one was open for 18% -> 20% of each run, Pallas kernels for 0% -> 0%
where the time goes in v1:
time: 69.3 us; the launch traced here: 68.9 us
  waiting for transfers between devices  22.6 us (33%)
  matrix products  19.7 us (28%)
  starting transfers between devices  15.6 us (23%)
  other arithmetic  5.23 us (8%)
  local copies, waits for them, and re-layouts  5.02 us (7%)
  between operations  0.8 us (1%)
    ppermute x12, waiting for transfers between devices, swap(): return lax.ppermute(value, AXES, pairs)  22.6 us
    ppermute x12, starting transfers between devices, swap(): return lax.ppermute(value, AXES, pairs)  15.6 us
    dot_general x3, matrix products, contract_first(): lax.dot_general(left_op, right_op, (((0,), (0,)), ((), ())), preferred_el...  12.1 us
    dot_general x2, matrix products, contract_inner(): return jnp.dot(left_op, right_op, preferred_element_type=jnp.float32)  3.99 us
    dot_general x3, matrix products, contract_last(): lax.dot_general(left_op, right_op, (((1,), (1,)), ((), ())), preferred_el...  3.59 us
    unnamed x10, local copies, waits for them, and re-layouts  2.84 us
    concatenate x2, local copies, waits for them, and re-layouts, all_rows(): jnp.concatenate([rows] + [swap(rows, mask, device_count) for mask in stag...  2.1 us
    unnamed x1, other arithmetic  1.45 us
  transfers between devices with their start and end apart: 12, of which 9 were waited for; matrix products, arithmetic and copies ran while one was open for 20% of the time, Pallas kernels for 0%

profile of v1, /device:TPU:0, one launch (start us, length us, event | category | flops | bytes accessed | tf_op | source)
XLA Modules:
  0.0 68.9 jit_solution(16472318729415462872)
XLA Ops:
  1.7 1.5 %constant_dynamic-update-slice_fusion.10 = (bf16[128,4224]{1,0:T(8,128)(2,1)}, bf16[256,4224]{1,0:T(8,128)(2,1)}, bf16[64,4224]{1,0:T(8,128)(2,1)S(1)}, bf16[8,4224]{1,0:T(8,128)(2,1)S(1)}) fusion(bf16[8,128]{1,0:T(8,128)(2,1)S(1)} %fusion.21, bf16[8,2048]{1,0:T(8,128)(2,1)} %param.8, bf16[8,2048]{1,0:T(8,128)(2,1)} %param.7), kind=kLoop, calls=%fused_computation.41 | loop fusion | flops 202749 | bytes 337920
  3.1 4.1 %collective-permute-start.1 = (bf16[8,4224]{1,0:T(8,128)(2,1)S(1)}, bf16[8,4224]{1,0:T(8,128)(2,1)S(1)}, u32[]{:S(2)}, u32[]{:S(2)}) collective-permute-start(bf16[8,4224]{1,0:T(8,128)(2,1)S(1)} %get-tuple-element.26), channel_id=1, source_target_pairs={{0,8},{1,9},{2,10},{3,11},{4,12},{5,13},{6,14},{7,15},{8,0},{9,1},... | collective-permute-start | bytes 202760 | tf_op jit(solution)/shard_map/ppermute | solution.py:48
  7.2 1.6 %collective-permute-start = (bf16[8,4224]{1,0:T(8,128)(2,1)S(1)}, bf16[8,4224]{1,0:T(8,128)(2,1)S(1)}, u32[]{:S(2)}, u32[]{:S(2)}) collective-permute-start(bf16[8,4224]{1,0:T(8,128)(2,1)S(1)} %get-tuple-element.26), channel_id=1, source_target_pairs={{0,4},{1,5},{2,6},{3,7},{4,0},{5,1},{6,2},{7,3},{8,12},{9,13},{10,... | collective-permute-start | bytes 202760 | tf_op jit(solution)/shard_map/ppermute | solution.py:48
  8.8 1.5 %collective-permute-done.1 = bf16[8,4224]{1,0:T(8,128)(2,1)S(1)} collective-permute-done((bf16[8,4224]{1,0:T(8,128)(2,1)S(1)}, bf16[8,4224]{1,0:T(8,128)(2,1)S(1)}, u32[]{:S(2)}, u32[]{:S(2)}) %collective-permute-start.1) | collective-permute-done | bytes 67616 | tf_op jit(solution)/shard_map/ppermute | solution.py:48
  10.3 1.2 %collective-permute-done = bf16[8,4224]{1,0:T(8,128)(2,1)S(1)} collective-permute-done((bf16[8,4224]{1,0:T(8,128)(2,1)S(1)}, bf16[8,4224]{1,0:T(8,128)(2,1)S(1)}, u32[]{:S(2)}, u32[]{:S(2)}) %collective-permute-start) | collective-permute-done | bytes 67616 | tf_op jit(solution)/shard_map/ppermute | solution.py:48
  11.5 3.4 %collective-permute-done.2 = bf16[8,4224]{1,0:T(8,128)(2,1)S(1)} collective-permute-done((bf16[8,4224]{1,0:T(8,128)(2,1)S(1)}, bf16[8,4224]{1,0:T(8,128)(2,1)S(1)}, u32[]{:S(2)}, u32[]{:S(2)}) %collective-permute-start.2) | collective-permute-done | bytes 67616 | tf_op jit(solution)/shard_map/ppermute | solution.py:48
  15.7 1.6 %collective-permute-start.3 = (bf16[32,4224]{1,0:T(8,128)(2,1)S(1)}, bf16[32,4224]{1,0:T(8,128)(2,1)S(1)}, u32[]{:S(2)}, u32[]{:S(2)}) collective-permute-start(bf16[32,4224]{1,0:T(8,128)(2,1)S(1)} %pad_maximum_fusion), channel_id=1, source_target_pairs={{0,2},{1,17},{2,0},{3,19},{4,6},{5,21},{6,4},{7,23},{8,10},{9,25},... | collective-permute-start | bytes 811016 | tf_op jit(solution)/shard_map/ppermute | solution.py:48
  19.2 3.0 %collective-permute-done.3 = bf16[32,4224]{1,0:T(8,128)(2,1)S(1)} collective-permute-done((bf16[32,4224]{1,0:T(8,128)(2,1)S(1)}, bf16[32,4224]{1,0:T(8,128)(2,1)S(1)}, u32[]{:S(2)}, u32[]{:S(2)}) %collective-permute-start.3) | collective-permute-done | bytes 270368 | tf_op jit(solution)/shard_map/ppermute | solution.py:48
  23.0 1.5 %collective-permute-start.4 = (bf16[64,4224]{1,0:T(8,128)(2,1)S(1)}, bf16[64,4224]{1,0:T(8,128)(2,1)S(1)}, u32[]{:S(2)}, u32[]{:S(2)}) collective-permute-start(bf16[64,4224]{1,0:T(8,128)(2,1)S(1)} %get-tuple-element.10), channel_id=1, source_target_pairs={{0,16},{1,3},{2,18},{3,1},{4,20},{5,7},{6,22},{7,5},{8,24},{9,11},... | collective-permute-start | bytes 1622024 | tf_op jit(solution)/shard_map/ppermute | solution.py:48
  24.5 7.9 %collective-permute-done.4 = bf16[64,4224]{1,0:T(8,128)(2,1)S(1)} collective-permute-done((bf16[64,4224]{1,0:T(8,128)(2,1)S(1)}, bf16[64,4224]{1,0:T(8,128)(2,1)S(1)}, u32[]{:S(2)}, u32[]{:S(2)}) %collective-permute-start.4) | collective-permute-done | bytes 540704 | tf_op jit(solution)/shard_map/ppermute | solution.py:48
  32.4 1.0 %constant_dynamic-update-slice_fusion.5 = (bf16[128,4224]{1,0:T(8,128)(2,1)}, bf16[256,4224]{1,0:T(8,128)(2,1)}) fusion(bf16[128,4224]{1,0:T(8,128)(2,1)} %get-tuple-element.8, bf16[64,4224]{1,0:T(8,128)(2,1)S(1)} %collective-permute-done.4, bf16[256,4224]{1,0:T(8,128)(2,1)} %get-tuple-element.9), kind=kLoop, calls=%fused_computation.36 | loop fusion | bytes 1622016 | tf_op jit(solution)/shard_map/concatenate | solution.py:71
  33.4 2.9 %collective-permute-done.5 = bf16[128,4224]{1,0:T(8,128)(2,1)S(1)} collective-permute-done((bf16[128,4224]{1,0:T(8,128)(2,1)}, bf16[128,4224]{1,0:T(8,128)(2,1)S(1)}, u32[]{:S(2)}, u32[]{:S(2)}) %collective-permute-start.5) | collective-permute-done | bytes 1081376 | tf_op jit(solution)/shard_map/ppermute | solution.py:48
  36.4 1.1 %constant_dynamic-update-slice_fusion.11 = bf16[256,4224]{1,0:T(8,128)(2,1)} fusion(bf16[256,4224]{1,0:T(8,128)(2,1)} %get-tuple-element.7, bf16[128,4224]{1,0:T(8,128)(2,1)S(1)} %collective-permute-done.5), kind=kLoop, calls=%fused_computation.42 | loop fusion | bytes 2162688 | tf_op jit(solution)/shard_map/concatenate | solution.py:71
  37.4 1.1 %select_reduce_fusion = f32[256]{0:T(256)S(1)} fusion(bf16[256,4224]{1,0:T(8,128)(2,1)} %constant_dynamic-update-slice_fusion.11, pred[128]{0:T(512)(128)(4,1)S(1)} %compare_and_fusion), kind=kLoop, calls=%fused_computation.28 | loop fusion | flops 98048 | bytes 66688 | tf_op jit(solution)/shard_map/reduce_sum | solution.py:76
  38.5 1.9 %fusion.3 = f32[256,512]{1,0:T(8,128)S(1)} fusion(bf16[1,2048,512]{2,1,0:T(8,128)(2,1)S(1)} %copy-done, bf16[256,4224]{1,0:T(8,128)(2,1)} %constant_dynamic-update-slice_fusion.11), kind=kOutput, calls=%fused_computation.7 | convolution fusion | flops 536870912 | bytes 3670016 | tf_op jit(solution)/shard_map/dot_general | solution.py:22
  40.5 2.1 %fusion.6 = f32[256,512]{1,0:T(8,128)S(1)} fusion(bf16[1,2048,512]{2,1,0:T(8,128)(2,1)S(1)} %copy-done.1, bf16[256,4224]{1,0:T(8,128)(2,1)} %constant_dynamic-update-slice_fusion.11), kind=kOutput, calls=%fused_computation.10 | convolution fusion | flops 536870912 | bytes 3670016 | tf_op jit(solution)/shard_map/dot_general | solution.py:22
  42.6 2.1 %multiply_convert_fusion.2 = (bf16[256,512]{1,0:T(8,128)(2,1)S(1)}, bf16[256,512]{1,0:T(8,128)(2,1)S(1)}) fusion(f32[256,512]{1,0:T(8,128)S(1)} %fusion.3, f32[256,512]{1,0:T(8,128)S(1)} %fusion.6, bf16[1,512,2048]{2,1,0:T(8,128)(2,1)S(1)} %copy-done.2, bf16[256,4224]{1,0:T(8,128)(2,1)} %constant_dynamic-update-slice_fusion.11, f32[256]{0:T(256)S(1)} %select_reduce_fusion), kind=kOutput, calls=%fused_computation.22 | convolution fusion | flops 540147712 | bytes 4719616 | tf_op jit(solution)/shard_map/dot_general | solution.py:10
  46.4 1.8 %collective-permute-done.6 = bf16[128,2048]{1,0:T(8,128)(2,1)S(1)} collective-permute-done((bf16[128,2048]{1,0:T(8,128)(2,1)S(1)}, bf16[128,2048]{1,0:T(8,128)(2,1)S(1)}, u32[]{:S(2)}, u32[]{:S(2)}) %collective-permute-start.6) | collective-permute-done | bytes 524320 | tf_op jit(solution)/shard_map/ppermute | solution.py:48
  48.4 1.6 %collective-permute-start.7 = (bf16[64,2048]{1,0:T(8,128)(2,1)S(1)}, bf16[64,2048]{1,0:T(8,128)(2,1)S(1)}, u32[]{:S(2)}, u32[]{:S(2)}) collective-permute-start(bf16[64,2048]{1,0:T(8,128)(2,1)S(1)} %split.43), channel_id=1, source_target_pairs={{0,16},{1,3},{2,18},{3,1},{4,20},{5,7},{6,22},{7,5},{8,24},{9,11},... | collective-permute-start | bytes 786440 | tf_op jit(solution)/shard_map/ppermute | solution.py:48
  49.9 4.1 %convolution_bitcast_fusion = f32[1,512,2048]{2,1,0:T(8,128)} fusion(bf16[256,4224]{1,0:T(8,128)(2,1)} %constant_dynamic-update-slice_fusion.11, f32[256]{0:T(256)S(1)} %select_reduce_fusion, f32[256,512]{1,0:T(8,128)S(1)} %fusion.6, f32[256,512]{1,0:T(8,128)S(1)} %fusion.3), kind=kOutput, calls=%fused_computation | convolution fusion | flops 539230208 | bytes 6292480 | tf_op jit(solution)/shard_map/dot_general | solution.py:16
  54.9 1.6 %collective-permute-start.8 = (bf16[32,2048]{1,0:T(8,128)(2,1)S(1)}, bf16[32,2048]{1,0:T(8,128)(2,1)S(1)}, u32[]{:S(2)}, u32[]{:S(2)}) collective-permute-start(bf16[32,2048]{1,0:T(8,128)(2,1)S(1)} %split.45), channel_id=1, source_target_pairs={{0,2},{1,17},{2,0},{3,19},{4,6},{5,21},{6,4},{7,23},{8,10},{9,25},... | collective-permute-start | bytes 393224 | tf_op jit(solution)/shard_map/ppermute | solution.py:48
  56.5 4.0 %convolution_bitcast_fusion.1 = f32[1,2048,512]{2,1,0:T(8,128)} fusion(bf16[256,512]{1,0:T(8,128)(2,1)S(1)} %get-tuple-element.4, bf16[256,4224]{1,0:T(8,128)(2,1)} %constant_dynamic-update-slice_fusion.11), kind=kOutput, calls=%fused_computation.1 | convolution fusion | flops 536870912 | bytes 5505024 | tf_op jit(solution)/shard_map/dot_general | solution.py:16
  60.6 2.9 %collective-permute-start.11 = (bf16[8,2048]{1,0:T(8,128)(2,1)S(1)}, bf16[8,2048]{1,0:T(8,128)(2,1)S(1)}, u32[]{:S(2)}, u32[]{:S(2)}) collective-permute-start(bf16[8,2048]{1,0:T(8,128)(2,1)S(1)} %get-tuple-element.12), channel_id=1, source_target_pairs={{0,12},{1,13},{2,14},{3,15},{4,8},{5,9},{6,10},{7,11},{8,4},{9,5},... | collective-permute-start | bytes 98312 | tf_op jit(solution)/shard_map/ppermute | solution.py:48
  64.1 4.0 %convolution_bitcast_fusion.2 = f32[1,2048,512]{2,1,0:T(8,128)} fusion(bf16[256,512]{1,0:T(8,128)(2,1)S(1)} %get-tuple-element.5, bf16[256,4224]{1,0:T(8,128)(2,1)} %constant_dynamic-update-slice_fusion.11), kind=kOutput, calls=%fused_computation.2 | convolution fusion | flops 536870912 | bytes 5505024 | tf_op jit(solution)/shard_map/dot_general | solution.py:16
  (35 shorter events, 8.9 us)
Async XLA Ops:
  0.6 37.9 %copy-start = (bf16[1,2048,512]{2,1,0:T(8,128)(2,1)S(1)}, bf16[1,2048,512]{2,1,0:T(8,128)(2,1)}, u32[]{:S(2)}) copy-start(bf16[1,2048,512]{2,1,0:T(8,128)(2,1)} %param.11) | copy-start | bytes 6291460
  3.1 7.2 %collective-permute-start.1 = (bf16[8,4224]{1,0:T(8,128)(2,1)S(1)}, bf16[8,4224]{1,0:T(8,128)(2,1)S(1)}, u32[]{:S(2)}, u32[]{:S(2)}) collective-permute-start(bf16[8,4224]{1,0:T(8,128)(2,1)S(1)} %get-tuple-element.26), channel_id=1, source_target_pairs={{0,8},{1,9},{2,10},{3,11},{4,12},{5,13},{6,14},{7,15},{8,0},{9,1},... | collective-permute-start | bytes 202760 | tf_op jit(solution)/shard_map/ppermute | solution.py:48
  7.2 4.3 %collective-permute-start = (bf16[8,4224]{1,0:T(8,128)(2,1)S(1)}, bf16[8,4224]{1,0:T(8,128)(2,1)S(1)}, u32[]{:S(2)}, u32[]{:S(2)}) collective-permute-start(bf16[8,4224]{1,0:T(8,128)(2,1)S(1)} %get-tuple-element.26), channel_id=1, source_target_pairs={{0,4},{1,5},{2,6},{3,7},{4,0},{5,1},{6,2},{7,3},{8,12},{9,13},{10,... | collective-permute-start | bytes 202760 | tf_op jit(solution)/shard_map/ppermute | solution.py:48
  8.8 6.1 %collective-permute-start.2 = (bf16[8,4224]{1,0:T(8,128)(2,1)S(1)}, bf16[8,4224]{1,0:T(8,128)(2,1)S(1)}, u32[]{:S(2)}, u32[]{:S(2)}) collective-permute-start(bf16[8,4224]{1,0:T(8,128)(2,1)S(1)} %get-tuple-element.26), channel_id=1, source_target_pairs={{0,12},{1,13},{2,14},{3,15},{4,8},{5,9},{6,10},{7,11},{8,4},{9,5},... | collective-permute-start | bytes 202760 | tf_op jit(solution)/shard_map/ppermute | solution.py:48
  15.7 6.5 %collective-permute-start.3 = (bf16[32,4224]{1,0:T(8,128)(2,1)S(1)}, bf16[32,4224]{1,0:T(8,128)(2,1)S(1)}, u32[]{:S(2)}, u32[]{:S(2)}) collective-permute-start(bf16[32,4224]{1,0:T(8,128)(2,1)S(1)} %pad_maximum_fusion), channel_id=1, source_target_pairs={{0,2},{1,17},{2,0},{3,19},{4,6},{5,21},{6,4},{7,23},{8,10},{9,25},... | collective-permute-start | bytes 811016 | tf_op jit(solution)/shard_map/ppermute | solution.py:48
  23.0 9.4 %collective-permute-start.4 = (bf16[64,4224]{1,0:T(8,128)(2,1)S(1)}, bf16[64,4224]{1,0:T(8,128)(2,1)S(1)}, u32[]{:S(2)}, u32[]{:S(2)}) collective-permute-start(bf16[64,4224]{1,0:T(8,128)(2,1)S(1)} %get-tuple-element.10), channel_id=1, source_target_pairs={{0,16},{1,3},{2,18},{3,1},{4,20},{5,7},{6,22},{7,5},{8,24},{9,11},... | collective-permute-start | bytes 1622024 | tf_op jit(solution)/shard_map/ppermute | solution.py:48
  33.4 2.9 %collective-permute-start.5 = (bf16[128,4224]{1,0:T(8,128)(2,1)}, bf16[128,4224]{1,0:T(8,128)(2,1)S(1)}, u32[]{:S(2)}, u32[]{:S(2)}) collective-permute-start(bf16[128,4224]{1,0:T(8,128)(2,1)} %get-tuple-element.6), channel_id=1, source_target_pairs={{0,1},{1,0},{2,3},{3,2},{4,5},{5,4},{6,7},{7,6},{8,9},{9,8},{10,11... | collective-permute-start | bytes 3244040 | tf_op jit(solution)/shard_map/ppermute | solution.py:48
  37.4 3.0 %copy-start.1 = (bf16[1,2048,512]{2,1,0:T(8,128)(2,1)S(1)}, bf16[1,2048,512]{2,1,0:T(8,128)(2,1)}, u32[]{:S(2)}) copy-start(bf16[1,2048,512]{2,1,0:T(8,128)(2,1)} %param.12) | copy-start | bytes 6291460
  40.5 2.1 %copy-start.2 = (bf16[1,512,2048]{2,1,0:T(8,128)(2,1)S(1)}, bf16[1,512,2048]{2,1,0:T(8,128)(2,1)}, u32[]{:S(2)}) copy-start(bf16[1,512,2048]{2,1,0:T(8,128)(2,1)} %param.13) | copy-start | bytes 6291460
  46.2 2.0 %collective-permute-start.6 = (bf16[128,2048]{1,0:T(8,128)(2,1)S(1)}, bf16[128,2048]{1,0:T(8,128)(2,1)S(1)}, u32[]{:S(2)}, u32[]{:S(2)}) collective-permute-start(bf16[128,2048]{1,0:T(8,128)(2,1)S(1)} %split.41), channel_id=1, source_target_pairs={{0,1},{1,0},{2,3},{3,2},{4,5},{5,4},{6,7},{7,6},{8,9},{9,8},{10,11... | collective-permute-start | bytes 1572872 | tf_op jit(solution)/shard_map/ppermute | solution.py:48
  48.4 6.4 %collective-permute-start.7 = (bf16[64,2048]{1,0:T(8,128)(2,1)S(1)}, bf16[64,2048]{1,0:T(8,128)(2,1)S(1)}, u32[]{:S(2)}, u32[]{:S(2)}) collective-permute-start(bf16[64,2048]{1,0:T(8,128)(2,1)S(1)} %split.43), channel_id=1, source_target_pairs={{0,16},{1,3},{2,18},{3,1},{4,20},{5,7},{6,22},{7,5},{8,24},{9,11},... | collective-permute-start | bytes 786440 | tf_op jit(solution)/shard_map/ppermute | solution.py:48
  54.9 5.6 %collective-permute-start.8 = (bf16[32,2048]{1,0:T(8,128)(2,1)S(1)}, bf16[32,2048]{1,0:T(8,128)(2,1)S(1)}, u32[]{:S(2)}, u32[]{:S(2)}) collective-permute-start(bf16[32,2048]{1,0:T(8,128)(2,1)S(1)} %split.45), channel_id=1, source_target_pairs={{0,2},{1,17},{2,0},{3,19},{4,6},{5,21},{6,4},{7,23},{8,10},{9,25},... | collective-permute-start | bytes 393224 | tf_op jit(solution)/shard_map/ppermute | solution.py:48
  60.5 7.5 %collective-permute-start.9 = (bf16[8,2048]{1,0:T(8,128)(2,1)S(1)}, bf16[8,2048]{1,0:T(8,128)(2,1)S(1)}, u32[]{:S(2)}, u32[]{:S(2)}) collective-permute-start(bf16[8,2048]{1,0:T(8,128)(2,1)S(1)} %get-tuple-element.11), channel_id=1, source_target_pairs={{0,4},{1,5},{2,6},{3,7},{4,0},{5,1},{6,2},{7,3},{8,12},{9,13},{10,... | collective-permute-start | bytes 98312 | tf_op jit(solution)/shard_map/ppermute | solution.py:48
  60.6 7.5 %collective-permute-start.11 = (bf16[8,2048]{1,0:T(8,128)(2,1)S(1)}, bf16[8,2048]{1,0:T(8,128)(2,1)S(1)}, u32[]{:S(2)}, u32[]{:S(2)}) collective-permute-start(bf16[8,2048]{1,0:T(8,128)(2,1)S(1)} %get-tuple-element.12), channel_id=1, source_target_pairs={{0,12},{1,13},{2,14},{3,15},{4,8},{5,9},{6,10},{7,11},{8,4},{9,5},... | collective-permute-start | bytes 98312 | tf_op jit(solution)/shard_map/ppermute | solution.py:48
  63.5 4.8 %collective-permute-start.10 = (bf16[8,2048]{1,0:T(8,128)(2,1)S(1)}, bf16[8,2048]{1,0:T(8,128)(2,1)S(1)}, u32[]{:S(2)}, u32[]{:S(2)}) collective-permute-start(bf16[8,2048]{1,0:T(8,128)(2,1)S(1)} %get-tuple-element.13), channel_id=1, source_target_pairs={{0,8},{1,9},{2,10},{3,11},{4,12},{5,13},{6,14},{7,15},{8,0},{9,1},... | collective-permute-start | bytes 98312 | tf_op jit(solution)/shard_map/ppermute | solution.py:48
